TPU v7x, 32 devices: a whole 2x2x4 slice. The times are simulated.
32 devices in a mesh: groups: 2 (over y), ep: 4 (over z), tp: 4 (over x, core).
Axes of the slice: x: 2, y: 2, z: 4, core: 2. Of those that a mesh axis runs over, the one named last changes fastest.
Arguments:
- context: bfloat16 [512, 4096], P(('groups', 'ep'), 'tp'), parts along dimension 0, may hold values from -6 to 6
- stream: bfloat16 [512, 4096], P(('groups', 'ep'), 'tp'), parts along dimension 0, may hold values from -14 to 14
- out_proj: bfloat16 [4096, 4096], P('tp', 'ep'), may hold values from -0.09375 to 0.09375
- norm_gain: bfloat16 [4096], P('tp'), may hold values from 0.099609375 to 1.8984375
- router: bfloat16 [4096, 4], P('tp'), may hold values from -0.0625 to 0.0625
- expert_ids: int32 [512, 2], P(('groups', 'ep')), parts along dimension 0, may hold values from 0 to 3, all different within a row; in each aligned block of 64 rows (0 to 63, 64 to 127, ...) at most 36 rows name the same one
- w_gate: bfloat16 [4096, 28672], P('tp', 'ep'), may hold values from -0.09375 to 0.09375
- w_up: bfloat16 [4096, 28672], P('tp', 'ep'), may hold values from -0.09375 to 0.09375
- w_down: bfloat16 [28672, 4096], P('ep', 'tp'), may hold values from -0.125 to 0.125
Outputs:
- layer_out: bfloat16 [512, 4096], P(('groups', 'ep'), 'tp'), parts along dimension 0
There are 2 independent parts, one for each index of `groups`. A program takes and returns all parts, laid end to end along the dimension named above; an argument that names none is the same for every part. Nothing has to cross between parts.
Inputs may be any that keep to these rules, and one draw needn't show every extreme that they name: `expert_ids`: each row names 2 different experts. In each aligned block of 64 rows (the rows of one index of ep) no expert is named by more than 36 rows, and in some blocks one expert is named by exactly 36 rows.
All inputs are finite; a program needn't handle non-finite values.
Results may differ from a plain program's by a relative error of at most 0.02.
Values may be sent and summed in bfloat16 or wider, within the bound.
A program may use at most 128 MiB of HBM per device.

v0:
```python
import functools

import jax
import jax.numpy as jnp
from jax import lax
from jax.experimental import pallas as pl
from jax.experimental.pallas import tpu as pltpu
from jax.sharding import PartitionSpec as P

D = 4096
EXPERTS = 4
CAP = 36


def plain_device(context, stream, out_proj, norm_gain, router, expert_ids, w_gate, w_up, w_down):
    tok_rows = stream.shape[0]
    width_part = stream.shape[1]
    ep_count = lax.axis_size("ep")
    fanout = ep_count // EXPERTS
    columns = jnp.dot(
        lax.all_gather(context, "ep", axis=0, tiled=True),
        out_proj,
        preferred_element_type=jnp.float32,
    )
    head_part = lax.all_to_all(
        columns.astype(jnp.bfloat16), "ep", split_axis=0, concat_axis=1, tiled=True
    )
    attention = lax.psum_scatter(head_part, "tp", scatter_dimension=1, tiled=True).astype(
        jnp.float32
    )
    hstate = (stream.astype(jnp.float32) + attention).astype(jnp.bfloat16)
    hfloat = hstate.astype(jnp.float32)
    gain_vec = norm_gain.astype(jnp.float32)
    router_wide = router.astype(jnp.float32)
    squares = jnp.sum(hfloat * hfloat, axis=1)
    total_sq = lax.psum(squares, "tp")
    inverse = lax.rsqrt(total_sq / D + 1e-05)[:, None]
    normed = hfloat * inverse * gain_vec[None, :]
    logits = lax.psum(jnp.dot(normed, router_wide, precision=lax.Precision.HIGHEST), "tp")
    inputs = normed.astype(jnp.bfloat16)
    experts_range = jnp.arange(EXPERTS, dtype=jnp.int32)
    flat_ids = expert_ids.reshape(tok_rows * 2)
    onehot = (flat_ids[:, None] == experts_range[None, :]).astype(jnp.int32)
    before = jnp.cumsum(onehot, axis=0) - onehot
    slot_index = jnp.sum(before * onehot, axis=1)
    target = flat_ids * CAP + slot_index
    picked = onehot.reshape(tok_rows, 2, EXPERTS).astype(jnp.float32)
    chosen = jnp.sum(picked * logits[:, None, :], axis=2)
    leading = jax.nn.sigmoid(chosen[:, 0] - chosen[:, 1])
    weights = jnp.stack([leading, 1.0 - leading], axis=1)
    columns_all = jnp.arange(EXPERTS * CAP, dtype=jnp.int32)
    placement = (
        (target[:, None] == columns_all[None, :])
        .astype(jnp.float32)
        .reshape(tok_rows, 2, EXPERTS * CAP)
    )
    dispatch = jnp.sum(placement, axis=1)
    combine = jnp.sum(placement * weights[:, :, None], axis=1)
    sectioned = lax.dot_general(
        dispatch.astype(jnp.bfloat16),
        inputs,
        (((0,), (0,)), ((), ())),
        preferred_element_type=jnp.float32,
    ).astype(jnp.bfloat16)
    send_rows = jnp.broadcast_to(
        sectioned.reshape(EXPERTS, 1, CAP, width_part), (EXPERTS, fanout, CAP, width_part)
    ).reshape(ep_count, CAP, width_part)
    received = lax.all_to_all(send_rows, "ep", split_axis=0, concat_axis=0, tiled=True)
    slot_count = received.shape[1]
    flattened = received.reshape(ep_count * slot_count, width_part)
    gate_part = jnp.dot(flattened, w_gate, preferred_element_type=jnp.float32)
    up_part = jnp.dot(flattened, w_up, preferred_element_type=jnp.float32)
    gate_sum = lax.psum(gate_part.astype(jnp.bfloat16), "tp").astype(jnp.float32)
    up_sum = lax.psum(up_part.astype(jnp.bfloat16), "tp").astype(jnp.float32)
    hidden = (jax.nn.silu(gate_sum) * up_sum).astype(jnp.bfloat16)
    partial_value = jnp.dot(hidden, w_down, preferred_element_type=jnp.float32).astype(jnp.bfloat16)
    returned_rows = lax.all_to_all(
        partial_value.reshape(ep_count, slot_count, width_part),
        "ep",
        split_axis=0,
        concat_axis=0,
        tiled=True,
    )
    summed = jnp.sum(
        returned_rows.astype(jnp.float32).reshape(EXPERTS, fanout, CAP, width_part), axis=1
    ).reshape(EXPERTS * CAP, width_part)
    expert_mix = jnp.dot(combine, summed, precision=lax.Precision.HIGHEST)
    return (hfloat + expert_mix).astype(jnp.bfloat16)


MESH = pl.DeviceIdType.MESH
CHUNK = 256
LAG_SUM, LAG_PASS, LAG_DOWN = 4, 7, 9
WINDOW = 40
ALIGN = 8
VMEM_BYTES = 67043328


def fused_kernel(
    n_ep,
    n_tp,
    pieces,
    ctx_ref,
    stream_ref,
    gain_ref,
    router_ref,
    ids_ref,
    proj_hbm,
    gate_hbm,
    up_hbm,
    down_hbm,
    out_ref,
    proj,
    gate,
    up,
    down,
    ctx_all,
    part,
    part_in,
    halves,
    landed,
    hkeep,
    x_all,
    rows,
    side,
    side_all,
    inv_all,
    slot_all,
    inv_rows,
    chooser,
    mix,
    pair_out,
    pair_in,
    own_far,
    own_near,
    far_out,
    far_in,
    hid,
    acc,
    outb,
    ret,
    w_sem,
    ctx_send,
    ctx_recv,
    slot_send,
    slot_recv,
    part_send,
    part_recv,
    land_send,
    land_recv,
    side_send,
    side_recv,
    x_send,
    x_recv,
    inv_send,
    inv_recv,
    pair_send,
    pair_recv,
    far_send,
    far_recv,
    hx_send,
    hx_recv,
    hc_send,
    hc_recv,
    hf_send,
    hf_recv,
    ret_send,
    ret_recv,
):
    me = lax.axis_index("ep")
    lane = lax.axis_index("tp")
    core = lax.rem(lane, 2)
    side_x = lane // 2
    mate = 2 * side_x + (1 - core)
    across = 2 * (1 - side_x) + core
    tok, width = stream_ref.shape
    depth = n_tp * width
    quarter = gate.shape[1] // n_tp
    count = quarter // CHUNK
    total_steps = 2 * count
    slots = rows.shape[1]
    f32, bf16 = jnp.float32, jnp.bfloat16
    peers = (me, me + 1 - 2 * lax.rem(me, 2), lax.rem(me + 2, 4), 3 - me)

    loads = {}
    number = 0
    for name, src, dst in (("p", proj_hbm, proj), ("g", gate_hbm, gate), ("u", up_hbm, up), ("d", down_hbm, down)):
        step = src.shape[0] // pieces
        group = []
        for p in range(pieces):
            copy = pltpu.make_async_copy(
                src.at[pl.ds(p * step, step)], dst.at[pl.ds(p * step, step)], w_sem.at[number]
            )
            copy.start()
            group.append(copy)
            number += 1
        loads[name] = group

    barrier = pltpu.get_barrier_semaphore()
    for de in range(n_ep):
        for dt in range(n_tp):
            if de or dt:
                pl.semaphore_signal(
                    barrier,
                    inc=1,
                    device_id={"ep": lax.rem(me + de, n_ep), "tp": lax.rem(lane + dt, n_tp)},
                    device_id_type=MESH,
                )

    experts = lax.broadcasted_iota(jnp.int32, (128, tok), 0)
    is_first = jnp.transpose(jnp.where(ids_ref[0:1, :] == experts, 1.0, 0.0).astype(f32))
    is_second = jnp.transpose(jnp.where(ids_ref[1:2, :] == experts, 1.0, 0.0).astype(f32))
    named = is_first + is_second
    lanes = lax.broadcasted_iota(jnp.int32, (tok, 128), 1)
    row_i = lax.broadcasted_iota(jnp.int32, (tok, tok), 0)
    col_i = lax.broadcasted_iota(jnp.int32, (tok, tok), 1)
    lower = jnp.where(col_i < row_i, 1.0, 0.0).astype(bf16)
    rank = jnp.dot(lower, named.astype(bf16), preferred_element_type=f32)
    slot_all[0] = jnp.where(named > 0.5, rank, -4096.0)

    pl.semaphore_wait(barrier, n_ep * n_tp - 1)

    def over_ep(src, dst, sends, recvs):
        copies = []
        for k in range(1, n_ep):
            copy = pltpu.make_async_remote_copy(
                src_ref=src,
                dst_ref=dst.at[k],
                send_sem=sends.at[k - 1],
                recv_sem=recvs.at[k - 1],
                device_id={"ep": peers[k]},
                device_id_type=MESH,
            )
            copy.start()
            copies.append(copy)
        return copies

    ctx_copies = over_ep(ctx_ref, ctx_all, ctx_send, ctx_recv)
    slot_copies = over_ep(slot_all.at[0], slot_all, slot_send, slot_recv)

    for copy in loads["p"]:
        copy.wait()
    part_copies, land_copies = [], []
    for i in range(2):
        pair = me // 2 if i == 0 else 1 - me // 2
        for k in (2 * i, 2 * i + 1):
            if k:
                ctx_copies[k - 1].wait_recv()
                value = ctx_all[k]
            else:
                value = ctx_ref[...]
            part[peers[k]] = jnp.dot(value, proj[...], preferred_element_type=f32).astype(bf16)
        copy = pltpu.make_async_remote_copy(
            src_ref=part.at[2 * pair + (1 - core)],
            dst_ref=part_in.at[i],
            send_sem=part_send.at[i],
            recv_sem=part_recv.at[i],
            device_id={"tp": mate},
            device_id_type=MESH,
        )
        copy.start()
        part_copies.append(copy)
        block = 2 * pair + core
        copy.wait_recv()
        halves[i] = (part[block].astype(f32) + part_in[i].astype(f32)).astype(bf16)
        copy = pltpu.make_async_remote_copy(
            src_ref=halves.at[i],
            dst_ref=landed.at[side_x],
            send_sem=land_send.at[i],
            recv_sem=land_recv.at[side_x],
            device_id={"ep": block, "tp": me},
            device_id_type=MESH,
        )
        here = jnp.logical_and(block == me, me == lane)

        @pl.when(here)
        def _():
            landed[side_x] = halves[i]

        @pl.when(jnp.logical_not(here))
        def _():
            copy.start()

        land_copies.append((copy, here))

    for j in range(2):
        source = 2 * j + lax.rem(me, 2)
        mine = jnp.logical_and(me == lane, source == lane)

        @pl.when(jnp.logical_not(mine))
        def _():
            pltpu.make_async_remote_copy(
                src_ref=halves.at[0],
                dst_ref=landed.at[j],
                send_sem=land_send.at[0],
                recv_sem=land_recv.at[j],
                device_id={"tp": mate},
                device_id_type=MESH,
            ).wait_recv()

    attention = landed[0].astype(f32) + landed[1].astype(f32)
    hstate = (stream_ref[...].astype(f32) + attention).astype(bf16)
    hkeep[...] = hstate
    hfloat = hstate.astype(f32)
    scaled = hfloat * gain_ref[...].astype(f32).reshape(1, width)
    x_all[0] = scaled.astype(bf16)
    x_copies = over_ep(x_all.at[0], x_all, x_send, x_recv)

    side[...] = jnp.zeros_like(side)
    side[:, 0:EXPERTS] = lax.dot_general(
        scaled,
        router_ref[...].astype(f32),
        (((1,), (1,)), ((), ())),
        precision=lax.Precision.HIGHEST,
        preferred_element_type=f32,
    )
    side[:, EXPERTS : EXPERTS + 1] = jnp.sum(hfloat * hfloat, axis=1, keepdims=True)
    side_copies = []
    for k in range(1, n_tp):
        copy = pltpu.make_async_remote_copy(
            src_ref=side,
            dst_ref=side_all.at[k - 1],
            send_sem=side_send.at[k - 1],
            recv_sem=side_recv.at[k - 1],
            device_id={"tp": lax.rem(lane + k, n_tp)},
            device_id_type=MESH,
        )
        copy.start()
        side_copies.append(copy)
    total = side[...]
    for k in range(1, n_tp):
        side_copies[k - 1].wait_recv()
        total = total + side_all[k - 1]
    inverse = lax.rsqrt(total[:, EXPERTS : EXPERTS + 1] / depth + 1e-05)
    logits = total * inverse
    first = jnp.sum(is_first * logits, axis=1, keepdims=True)
    second = jnp.sum(is_second * logits, axis=1, keepdims=True)
    leading = jax.nn.sigmoid(first - second)
    mix[...] = is_first * leading + is_second * (1.0 - leading)
    inv_all[0] = jnp.broadcast_to(inverse, (tok, 128))
    inv_copies = over_ep(inv_all.at[0], inv_all, inv_send, inv_recv)

    for copy in slot_copies:
        copy.wait_recv()
    wide = lanes.astype(f32)
    for g in range(2):
        columns = []
        for p in range(2):
            picked = jnp.sum(jnp.where(lanes == me, slot_all[2 * g + p], 0.0), axis=1, keepdims=True)
            columns.append(jnp.where(picked + float(p * CAP) == wide, 1.0, 0.0).astype(f32))
        chooser[g] = jnp.transpose(jnp.concatenate(columns, axis=0))[:slots]

    def fill_rows(g):
        rows[g] = jnp.dot(
            chooser[g].astype(bf16),
            x_all[2 * g : 2 * g + 2].reshape(2 * tok, width),
            preferred_element_type=f32,
        ).astype(bf16)

    def fill_inverse(g):
        inv_rows[g] = jnp.dot(
            chooser[g],
            inv_all[2 * g : 2 * g + 2].reshape(2 * tok, 128),
            precision=lax.Precision.HIGHEST,
            preferred_element_type=f32,
        )

    acc[...] = jnp.zeros_like(acc)
    for name in ("g", "u", "d"):
        for copy in loads[name]:
            copy.wait()
    x_copies[0].wait_recv()
    fill_rows(0)

    def ret_copy(k):
        return pltpu.make_async_remote_copy(
            src_ref=outb.at[k // 2, pl.ds((k % 2) * (CAP // ALIGN * ALIGN), WINDOW)],
            dst_ref=ret.at[k],
            send_sem=ret_send.at[k - 1],
            recv_sem=ret_recv.at[k - 1],
            device_id={"ep": peers[k]},
            device_id_type=MESH,
        )

    def pair_copy(i):
        return pltpu.make_async_remote_copy(
            src_ref=pair_out.at[i], dst_ref=pair_in.at[i], send_sem=pair_send.at[i], recv_sem=pair_recv.at[i],
            device_id={"tp": mate}, device_id_type=MESH,
        )

    def far_copy(i):
        return pltpu.make_async_remote_copy(
            src_ref=far_out.at[i], dst_ref=far_in.at[i], send_sem=far_send.at[i], recv_sem=far_recv.at[i],
            device_id={"tp": across}, device_id_type=MESH,
        )

    own_q = 2 * core + side_x
    far_q = 2 * core + (1 - side_x)

    def hid_copy(i, q, target, sends, recvs):
        return pltpu.make_async_remote_copy(
            src_ref=hid.at[q, i], dst_ref=hid.at[q, i], send_sem=sends.at[i], recv_sem=recvs.at[i],
            device_id={"tp": target}, device_id_type=MESH,
        )

    def columns_of(weight, q, i):
        return weight[:, pl.ds(pl.multiple_of(q * quarter + lax.rem(i, count) * CHUNK, CHUNK), CHUNK)]

    def step(s, carry):
        @pl.when(s == count)
        def _():
            for k in (2, 3):
                x_copies[k - 1].wait_recv()
            fill_rows(1)

        @pl.when(s < total_steps)
        def _():
            i = s
            value = rows[i // count]
            for j in range(2):
                for m, weight in enumerate((gate, up)):
                    pair_out[i, 2 * j + m] = jnp.dot(
                        value, columns_of(weight, 2 * (1 - core) + j, i), preferred_element_type=f32
                    ).astype(bf16)
            pair_copy(i).start()
            for m, weight in enumerate((gate, up)):
                own_far[lax.rem(i, 2), m] = jnp.dot(
                    value, columns_of(weight, far_q, i), preferred_element_type=f32
                )
                own_near[i, m] = jnp.dot(
                    value, columns_of(weight, own_q, i), preferred_element_type=f32
                )

        @pl.when(jnp.logical_and(s >= 1, s < total_steps + 1))
        def _():
            i = s - 1
            pair_copy(i).wait_recv()
            for m in range(2):
                far_out[i, m] = (
                    own_far[lax.rem(i, 2), m] + pair_in[i, 2 * (1 - side_x) + m].astype(f32)
                ).astype(bf16)
            far_copy(i).start()
            for m in range(2):
                own_near[i, m] = own_near[i, m] + pair_in[i, 2 * side_x + m].astype(f32)

        @pl.when(s == LAG_SUM)
        def _():
            inv_copies[0].wait_recv()
            fill_inverse(0)

        @pl.when(s == count + LAG_SUM)
        def _():
            for k in (2, 3):
                inv_copies[k - 1].wait_recv()
            fill_inverse(1)

        @pl.when(jnp.logical_and(s >= LAG_SUM, s < total_steps + LAG_SUM))
        def _():
            i = s - LAG_SUM
            far_copy(i).wait_recv()
            scale = inv_rows[i // count, :, 0:1]
            g = (own_near[i, 0] + far_in[i, 0].astype(f32)) * scale
            u = (own_near[i, 1] + far_in[i, 1].astype(f32)) * scale
            hid[own_q, i] = (g / (1.0 + jnp.exp(-g)) * u).astype(bf16)
            hid_copy(i, own_q, across, hx_send, hx_recv).start()
            hid_copy(i, own_q, mate, hc_send, hc_recv).start()

        @pl.when(jnp.logical_and(s >= LAG_PASS, s < total_steps + LAG_PASS))
        def _():
            i = s - LAG_PASS
            hid_copy(i, far_q, across, hx_send, hx_recv).wait_recv()
            hid_copy(i, far_q, mate, hf_send, hf_recv).start()

        @pl.when(s >= LAG_DOWN)
        def _():
            i = s - LAG_DOWN
            hid_copy(i, own_q, mate, hc_send, hc_recv).wait_recv()
            hid_copy(i, far_q, mate, hf_send, hf_recv).wait_recv()
            value = acc[...]
            for q in range(4):
                value = value + jnp.dot(
                    hid[q, i],
                    down[pl.ds(pl.multiple_of(q * quarter + lax.rem(i, count) * CHUNK, CHUNK), CHUNK), :],
                    preferred_element_type=f32,
                )
            acc[...] = value

            @pl.when(i == count - 1)
            def _():
                outb[0] = acc[...].astype(bf16)
                ret_copy(1).start()
                acc[...] = jnp.zeros_like(acc)

        return carry

    lax.fori_loop(0, total_steps + LAG_DOWN, step, 0)

    outb[1] = acc[...].astype(bf16)
    for k in (2, 3):
        ret_copy(k).start()
    window = lax.broadcasted_iota(jnp.int32, (tok, WINDOW), 1).astype(f32)

    def returned(k):
        at_source = lanes == peers[k]
        shift = float((k % 2) * (CAP - CAP // ALIGN * ALIGN))
        place = jnp.sum(jnp.where(at_source, slot_all[0], 0.0), axis=1, keepdims=True) + shift
        chosen = jnp.where(place == window, 1.0, 0.0).astype(bf16)
        weight = jnp.sum(jnp.where(at_source, mix[...], 0.0), axis=1, keepdims=True)
        value = outb[0, 0:WINDOW, :] if k == 0 else ret[k]
        return weight * jnp.dot(chosen, value, preferred_element_type=f32)

    mixed = hkeep[...].astype(f32) + returned(0)
    for k in range(1, n_ep):
        ret_copy(k).wait_recv()
        mixed = mixed + returned(k)
    out_ref[...] = mixed.astype(bf16)
    for k in range(1, n_ep):
        ret_copy(k).wait_send()

    for copy in ctx_copies + slot_copies + part_copies + side_copies + x_copies + inv_copies:
        copy.wait_send()
    for copy, here in land_copies:

        @pl.when(jnp.logical_not(here))
        def _():
            copy.wait_send()

    def drain(i, carry):
        pair_copy(i).wait_send()
        far_copy(i).wait_send()
        hid_copy(i, own_q, across, hx_send, hx_recv).wait_send()
        hid_copy(i, own_q, mate, hc_send, hc_recv).wait_send()
        hid_copy(i, far_q, mate, hf_send, hf_recv).wait_send()
        return carry

    lax.fori_loop(0, total_steps, drain, 0)


def fused_device(context, stream, out_proj, norm_gain, router, expert_ids, w_gate, w_up, w_down):
    n_ep, n_tp = lax.axis_size("ep"), lax.axis_size("tp")
    tok, width = stream.shape
    heads = context.shape[1]
    hidden = w_gate.shape[1]
    cols = out_proj.shape[1]
    slots = 2 * CAP
    count = 2 * (hidden // n_tp // CHUNK)
    pieces = 4
    bf16, f32 = jnp.bfloat16, jnp.float32
    vmem, hbm = pl.BlockSpec(memory_space=pltpu.VMEM), pl.BlockSpec(memory_space=pl.ANY)
    dma = lambda n: pltpu.SemaphoreType.DMA((n,))
    scratch = [
        pltpu.VMEM(out_proj.shape, bf16),
        pltpu.VMEM(w_gate.shape, bf16),
        pltpu.VMEM(w_up.shape, bf16),
        pltpu.VMEM(w_down.shape, bf16),
        pltpu.VMEM((n_ep, tok, heads), bf16),
        pltpu.VMEM((n_ep, tok, cols), bf16),
        pltpu.VMEM((2, tok, cols), bf16),
        pltpu.VMEM((2, tok, cols), bf16),
        pltpu.VMEM((2, tok, cols), bf16),
        pltpu.VMEM((tok, width), bf16),
        pltpu.VMEM((n_ep, tok, width), bf16),
        pltpu.VMEM((2, slots, width), bf16),
        pltpu.VMEM((tok, 128), f32),
        pltpu.VMEM((n_tp - 1, tok, 128), f32),
        pltpu.VMEM((n_ep, tok, 128), f32),
        pltpu.VMEM((n_ep, tok, 128), f32),
        pltpu.VMEM((2, slots, 128), f32),
        pltpu.VMEM((2, slots, 2 * tok), f32),
        pltpu.VMEM((tok, 128), f32),
        pltpu.VMEM((count, 4, slots, CHUNK), bf16),
        pltpu.VMEM((count, 4, slots, CHUNK), bf16),
        pltpu.VMEM((2, 2, slots, CHUNK), f32),
        pltpu.VMEM((count, 2, slots, CHUNK), f32),
        pltpu.VMEM((count, 2, slots, CHUNK), bf16),
        pltpu.VMEM((count, 2, slots, CHUNK), bf16),
        pltpu.VMEM((4, count, slots, CHUNK), bf16),
        pltpu.VMEM((slots, width), f32),
        pltpu.VMEM((2, slots, width), bf16),
        pltpu.VMEM((n_ep, WINDOW, width), bf16),
        dma(4 * pieces),
    ]
    for size in (n_ep - 1, n_ep - 1, 2, 2, n_tp - 1, n_ep - 1, n_ep - 1, count, count, count, count, count, n_ep - 1):
        scratch += [dma(size), dma(size)]
    return pl.pallas_call(
        functools.partial(fused_kernel, n_ep, n_tp, pieces),
        out_shape=jax.ShapeDtypeStruct((tok, width), bf16),
        in_specs=[vmem] * 5 + [hbm] * 4,
        out_specs=vmem,
        scratch_shapes=scratch,
        compiler_params=pltpu.CompilerParams(
            collective_id=0, has_side_effects=True, vmem_limit_bytes=VMEM_BYTES
        ),
        name="fused_layer",
    )(context, stream, norm_gain, router.T, expert_ids.T, out_proj, w_gate, w_up, w_down)


def solution(mesh):
    sizes = dict(mesh.shape)
    fused = sizes["tp"] == 4 and sizes["ep"] == EXPERTS
    return jax.shard_map(
        fused_device if fused else plain_device,
        mesh=mesh,
        in_specs=(
            P(("groups", "ep"), "tp"),
            P(("groups", "ep"), "tp"),
            P("tp", "ep"),
            P("tp"),
            P("tp", None),
            P(("groups", "ep"), None),
            P("tp", "ep"),
            P("tp", "ep"),
            P("ep", "tp"),
        ),
        out_specs=P(("groups", "ep"), "tp"),
        check_vma=False,
    )
```

profile of v0, /device:TPU:0, one launch (start us, length us, event | category | flops | bytes accessed | tf_op | source)
XLA Modules:
  0.0 89.2 jit_solution(6849066330750395271)
XLA Ops:
  0.0 87.6 %fused_layer.1 = bf16[64,1024]{1,0:T(8,128)(2,1)} custom-call(bf16[64,1024]{1,0:T(8,128)(2,1)} %ctx_ref.1, bf16[64,1024]{1,0:T(8,128)(2,1)} %stream_ref.1, bf16[1024]{0:T(1024)(128)(2,1)} %gain_ref.1, bf16[4,1024]{1,0:T(4,128)(2,1)} %bitcast.2, s32[2,64]{1,0:T(2,128)} %bitcast.3, bf16[1024,1024]{1,0:T(8,128)(2,1)} %proj_hbm.1, bf16[1024,7168]{1,0:T(8,128)(2,1)} %gate_hbm.1, ...), custom_call_target="tpu_custom_call" | custom-call | tf_op jit(solution)/shard_map/fused_layer/pallas_call | solution.py:585
  87.6 1.6 %copy.11 = bf16[64,1024]{1,0:T(8,128)(2,1)} copy(bf16[64,1024]{1,0:T(8,128)(2,1)} %fused_layer.1) | data formatting | bytes 262144
where the time goes:
time: 89.4 us; the launch traced here: 89.2 us
  Pallas kernels  87.6 us (98%)
  local copies, waits for them, and re-layouts  1.57 us (2%)
    pallas_call x1, Pallas kernels, fused_device(): pl.pallas_call(functools.partial(fused_kernel, n_ep, n_tp, pieces), out_s...  87.6 us

commit v1 on v0

v1 whole, which is shorter than its diff:
```python
import functools

import jax
import jax.numpy as jnp
from jax import lax
from jax.experimental import pallas as pl
from jax.experimental.pallas import tpu as pltpu
from jax.sharding import PartitionSpec as P

D = 4096
EXPERTS = 4
CAP = 36


def plain_device(context, stream, out_proj, norm_gain, router, expert_ids, w_gate, w_up, w_down):
    tok_rows = stream.shape[0]
    width_part = stream.shape[1]
    ep_count = lax.axis_size("ep")
    fanout = ep_count // EXPERTS
    columns = jnp.dot(
        lax.all_gather(context, "ep", axis=0, tiled=True),
        out_proj,
        preferred_element_type=jnp.float32,
    )
    head_part = lax.all_to_all(
        columns.astype(jnp.bfloat16), "ep", split_axis=0, concat_axis=1, tiled=True
    )
    attention = lax.psum_scatter(head_part, "tp", scatter_dimension=1, tiled=True).astype(
        jnp.float32
    )
    hstate = (stream.astype(jnp.float32) + attention).astype(jnp.bfloat16)
    hfloat = hstate.astype(jnp.float32)
    gain_vec = norm_gain.astype(jnp.float32)
    router_wide = router.astype(jnp.float32)
    squares = jnp.sum(hfloat * hfloat, axis=1)
    total_sq = lax.psum(squares, "tp")
    inverse = lax.rsqrt(total_sq / D + 1e-05)[:, None]
    normed = hfloat * inverse * gain_vec[None, :]
    logits = lax.psum(jnp.dot(normed, router_wide, precision=lax.Precision.HIGHEST), "tp")
    inputs = normed.astype(jnp.bfloat16)
    experts_range = jnp.arange(EXPERTS, dtype=jnp.int32)
    flat_ids = expert_ids.reshape(tok_rows * 2)
    onehot = (flat_ids[:, None] == experts_range[None, :]).astype(jnp.int32)
    before = jnp.cumsum(onehot, axis=0) - onehot
    slot_index = jnp.sum(before * onehot, axis=1)
    target = flat_ids * CAP + slot_index
    picked = onehot.reshape(tok_rows, 2, EXPERTS).astype(jnp.float32)
    chosen = jnp.sum(picked * logits[:, None, :], axis=2)
    leading = jax.nn.sigmoid(chosen[:, 0] - chosen[:, 1])
    weights = jnp.stack([leading, 1.0 - leading], axis=1)
    columns_all = jnp.arange(EXPERTS * CAP, dtype=jnp.int32)
    placement = (
        (target[:, None] == columns_all[None, :])
        .astype(jnp.float32)
        .reshape(tok_rows, 2, EXPERTS * CAP)
    )
    dispatch = jnp.sum(placement, axis=1)
    combine = jnp.sum(placement * weights[:, :, None], axis=1)
    sectioned = lax.dot_general(
        dispatch.astype(jnp.bfloat16),
        inputs,
        (((0,), (0,)), ((), ())),
        preferred_element_type=jnp.float32,
    ).astype(jnp.bfloat16)
    send_rows = jnp.broadcast_to(
        sectioned.reshape(EXPERTS, 1, CAP, width_part), (EXPERTS, fanout, CAP, width_part)
    ).reshape(ep_count, CAP, width_part)
    received = lax.all_to_all(send_rows, "ep", split_axis=0, concat_axis=0, tiled=True)
    slot_count = received.shape[1]
    flattened = received.reshape(ep_count * slot_count, width_part)
    gate_part = jnp.dot(flattened, w_gate, preferred_element_type=jnp.float32)
    up_part = jnp.dot(flattened, w_up, preferred_element_type=jnp.float32)
    gate_sum = lax.psum(gate_part.astype(jnp.bfloat16), "tp").astype(jnp.float32)
    up_sum = lax.psum(up_part.astype(jnp.bfloat16), "tp").astype(jnp.float32)
    hidden = (jax.nn.silu(gate_sum) * up_sum).astype(jnp.bfloat16)
    partial_value = jnp.dot(hidden, w_down, preferred_element_type=jnp.float32).astype(jnp.bfloat16)
    returned_rows = lax.all_to_all(
        partial_value.reshape(ep_count, slot_count, width_part),
        "ep",
        split_axis=0,
        concat_axis=0,
        tiled=True,
    )
    summed = jnp.sum(
        returned_rows.astype(jnp.float32).reshape(EXPERTS, fanout, CAP, width_part), axis=1
    ).reshape(EXPERTS * CAP, width_part)
    expert_mix = jnp.dot(combine, summed, precision=lax.Precision.HIGHEST)
    return (hfloat + expert_mix).astype(jnp.bfloat16)


MESH = pl.DeviceIdType.MESH
CHUNK = 256
PAD = (CAP + 7) // 8 * 8
SHIFT = PAD - CAP
PACK = 2 * CAP
BASE = PACK - PAD
HOLD = 2
LAG_SUM, LAG_PASS, LAG_DOWN = 4, 7, 9
RING = 14
PIECES = 4
VMEM_BYTES = 67043328


def packed(low, high):
    return jnp.concatenate([low[:BASE], low[BASE:] + high[: PAD - BASE], high[PAD - BASE :]], axis=0)


def fused_kernel(
    n_ep,
    n_tp,
    ctx_hbm,
    stream_hbm,
    gain_hbm,
    router_hbm,
    ids_hbm,
    proj_hbm,
    gate_hbm,
    up_hbm,
    down_hbm,
    out_ref,
    ctx_all,
    stream,
    gain,
    router,
    ids,
    proj,
    gate,
    up,
    down,
    disp,
    part,
    part_in,
    halves,
    landed,
    hkeep,
    x_out,
    x_all,
    x_high,
    side,
    side_all,
    named,
    inv_out,
    inv_all,
    cols,
    pair_out,
    pair_in,
    own_far,
    own_near,
    far_out,
    far_in,
    hid,
    acc,
    outb,
    ret,
    in_sem,
    w_sem,
    ctx_send,
    ctx_recv,
    part_send,
    part_recv,
    land_send,
    land_recv,
    side_send,
    side_recv,
    x_send,
    x_recv,
    inv_send,
    inv_recv,
    ret_send,
    ret_recv,
    loop_send,
    pair_recv,
    far_recv,
    hx_recv,
    hm_recv,
):
    me = lax.axis_index("ep")
    lane = lax.axis_index("tp")
    core = lax.rem(lane, 2)
    side_x = lane // 2
    mate = 2 * side_x + (1 - core)
    across = 2 * (1 - side_x) + core
    tok, width = stream.shape
    depth = n_tp * width
    quarter = gate.shape[1] // n_tp
    count = quarter // CHUNK
    units = n_ep * count
    half = width // 2
    f32, bf16 = jnp.float32, jnp.bfloat16
    peers = (me, me + 1 - 2 * lax.rem(me, 2), lax.rem(me + 2, 4), 3 - me)
    slot_of = (0, 3, 1, 2)
    peer_of = (0, 2, 3, 1)
    middle = lax.rem((me + 1) // 2, 2)
    far_k, next_k = 3 - middle, 2 + middle
    far_peer, next_peer = 3 * (1 - me // 2), 2 - me // 2

    barrier = pltpu.get_barrier_semaphore()
    for de in range(n_ep):
        for dt in range(n_tp):
            if de or dt:
                pl.semaphore_signal(
                    barrier,
                    inc=1,
                    device_id={"ep": lax.rem(me + de, n_ep), "tp": lax.rem(lane + dt, n_tp)},
                    device_id_type=MESH,
                )

    smalls = []
    for number, (src, dst) in enumerate(
        ((ctx_hbm, ctx_all.at[0]), (ids_hbm, ids), (stream_hbm, stream), (gain_hbm, gain), (router_hbm, router))
    ):
        copy = pltpu.make_async_copy(src, dst, in_sem.at[number])
        copy.start()
        smalls.append(copy)
    weights = []
    for number, (src, dst) in enumerate(((proj_hbm, proj), (gate_hbm, gate), (up_hbm, up), (down_hbm, down))):
        step_rows = src.shape[0] // PIECES
        for p in range(PIECES):
            rows = pl.ds(p * step_rows, step_rows)
            pltpu.make_async_copy(src.at[rows], dst.at[rows], w_sem.at[number]).start()
        weights.append(pltpu.make_async_copy(src, dst, w_sem.at[number]))

    smalls[1].wait()
    kinds = lax.broadcasted_iota(jnp.int32, (8, tok), 0)
    named[0] = jnp.where(ids[0:1, :] == kinds, 1.0, 0.0).astype(f32)
    named[1] = jnp.where(ids[1:2, :] == kinds, 1.0, 0.0).astype(f32)
    both = named[0] + named[1]
    row_i = lax.broadcasted_iota(jnp.int32, (tok, tok), 0)
    col_i = lax.broadcasted_iota(jnp.int32, (tok, tok), 1)
    earlier = jnp.where(row_i < col_i, 1.0, 0.0).astype(bf16)
    rank = jnp.dot(both.astype(bf16), earlier, preferred_element_type=f32)
    rank = jnp.where(both > 0.5, rank, -4096.0)
    named[2] = rank
    slots = lax.broadcasted_iota(jnp.int32, (PAD, tok), 0).astype(f32)

    def row_of(table, k):
        return jnp.sum(jnp.where(kinds == peers[k], table, 0.0), axis=0, keepdims=True)

    for g in range(4):
        disp[g * PAD : (g + 1) * PAD] = jnp.where(row_of(rank, peer_of[g]) == slots, 1.0, 0.0).astype(f32)
    disp[4 * PAD : 5 * PAD] = jnp.where(row_of(rank, 0) + float(SHIFT) == slots, 1.0, 0.0).astype(f32)
    side[...] = jnp.zeros_like(side)
    acc[...] = jnp.zeros_like(acc)

    smalls[0].wait()
    pl.semaphore_wait(barrier, n_ep * n_tp - 1)

    def ep_copy(src, dst, slot, send, recv, target):
        return pltpu.make_async_remote_copy(
            src_ref=src,
            dst_ref=dst.at[slot],
            send_sem=send,
            recv_sem=recv.at[slot],
            device_id={"ep": target},
            device_id_type=MESH,
        )

    def ctx_copy(n, k, target):
        return ep_copy(ctx_all.at[0], ctx_all, k, ctx_send.at[n], ctx_recv, target)

    ctx_sends = (ctx_copy(0, far_k, far_peer), ctx_copy(1, next_k, next_peer), ctx_copy(2, 1, peers[1]))
    for copy in ctx_sends:
        copy.start()
    weights[0].wait()

    order = (0, 1 + middle, 2 + middle, 3 - 2 * middle)
    owners = (
        me,
        (1 - middle) * peers[1] + middle * peers[2],
        (1 - middle) * peers[2] + middle * peers[3],
        (1 - middle) * peers[3] + middle * peers[1],
    )

    def part_copy(n):
        return pltpu.make_async_remote_copy(
            src_ref=part.at[n, 1 - core],
            dst_ref=part_in.at[n],
            send_sem=part_send.at[n],
            recv_sem=part_recv.at[n],
            device_id={"tp": mate},
            device_id_type=MESH,
        )

    def land_copy(n):
        return pltpu.make_async_remote_copy(
            src_ref=halves.at[n],
            dst_ref=landed.at[lane],
            send_sem=land_send.at[n],
            recv_sem=land_recv.at[lane],
            device_id={"ep": owners[n], "tp": me},
            device_id_type=MESH,
        )

    at_home = me == lane

    def finish_part(n):
        part_copy(n).wait_recv()
        halves[n] = (part[n, core].astype(f32) + part_in[n].astype(f32)).astype(bf16)
        if n:
            land_copy(n).start()
        else:

            @pl.when(at_home)
            def _():
                landed[lane] = halves[n]

            @pl.when(jnp.logical_not(at_home))
            def _():
                land_copy(n).start()

    for n in range(4):
        if n:
            ctx_copy(0, order[n], far_peer).wait_recv()
        value = ctx_all[order[n]]
        for h in range(2):
            part[n, h] = jnp.dot(
                value, proj[:, h * half : (h + 1) * half], preferred_element_type=f32
            ).astype(bf16)
        part_copy(n).start()
        if n:
            finish_part(n - 1)
    finish_part(3)

    smalls[2].wait()
    smalls[3].wait()
    smalls[4].wait()
    for t in range(n_tp):

        @pl.when(jnp.logical_not(jnp.logical_and(at_home, lane == t)))
        def _():
            pltpu.make_async_remote_copy(
                src_ref=halves.at[0],
                dst_ref=landed.at[t],
                send_sem=land_send.at[0],
                recv_sem=land_recv.at[t],
                device_id={"tp": mate},
                device_id_type=MESH,
            ).wait_recv()

    attention = jnp.concatenate(
        [landed[h].astype(f32) + landed[2 + h].astype(f32) for h in range(2)], axis=1
    )
    hstate = (stream[...].astype(f32) + attention).astype(bf16)
    hkeep[...] = hstate
    scaled = hstate.astype(f32) * gain[...].astype(f32).reshape(1, width)
    rows = jnp.dot(disp[...].astype(bf16), scaled.astype(bf16), preferred_element_type=f32).astype(bf16)
    x_all[0] = rows[:PAD]
    for g in range(1, 4):
        x_out[g] = rows[g * PAD : (g + 1) * PAD]
    x_high[0] = rows[4 * PAD : 5 * PAD]

    def x_copy(n, slot, target):
        return pltpu.make_async_remote_copy(
            src_ref=x_out.at[slot],
            dst_ref=x_all.at[slot],
            send_sem=x_send.at[n],
            recv_sem=x_recv.at[slot],
            device_id={"ep": target},
            device_id_type=MESH,
        )

    x_sends = (x_copy(0, far_k - 1, far_peer), x_copy(1, next_k - 1, next_peer), x_copy(2, 3, peers[1]))
    for copy in x_sends:
        copy.start()

    own_q = 2 * core + side_x
    far_q = 2 * core + (1 - side_x)

    def place_of(i):
        p = lax.rem(i + HOLD, units)
        return p // count, lax.rem(p, count)

    def tp_copy(src, dst, target, number, recv):
        return pltpu.make_async_remote_copy(
            src_ref=src,
            dst_ref=dst,
            send_sem=loop_send.at[number],
            recv_sem=recv,
            device_id={"tp": target},
            device_id_type=MESH,
        )

    def pair_copy(i):
        return tp_copy(pair_out.at[i], pair_in.at[i], mate, 0, pair_recv.at[lax.rem(i, RING)])

    def far_copy(i):
        return tp_copy(far_out.at[i], far_in.at[i], across, 1, far_recv.at[lax.rem(i, RING)])

    def hid_across(i, q):
        return tp_copy(hid.at[q, i], hid.at[q, i], across, 2, hx_recv.at[lax.rem(i, RING)])

    def hid_mate(i, q, number):
        return tp_copy(hid.at[q, i], hid.at[q, i], mate, number, hm_recv.at[lax.rem(i, RING)])

    def columns_of(weight, q, chunk):
        return weight[:, pl.ds(pl.multiple_of(q * quarter + chunk * CHUNK, CHUNK), CHUNK)]

    def multiply(i):
        group, chunk = place_of(i)
        low, high = x_all[group], x_high[group]

        def block(q):
            return packed(
                jnp.dot(low, columns_of(gate, q, chunk), preferred_element_type=f32),
                jnp.dot(high, columns_of(up, q, chunk), preferred_element_type=f32),
            )

        for j in range(2):
            pair_out[i, j] = block(2 * (1 - core) + j).astype(bf16)
        own_far[lax.rem(i, 2)] = block(far_q)
        own_near[i] = block(own_q)

    def pass_far(i):
        far_out[i] = (own_far[lax.rem(i, 2)] + pair_in[i, 1 - side_x].astype(f32)).astype(bf16)

    def activate(i):
        group, _ = place_of(i)
        total = own_near[i] + pair_in[i, side_x].astype(f32) + far_in[i].astype(f32)
        scale = inv_all[group][:, 0:1]
        g = total[:PAD] * scale
        u = pltpu.roll(total[BASE:], CAP, 0) * scale
        hid[own_q, i] = (g / (1.0 + jnp.exp(-g)) * u).astype(bf16)

    def descend(i):
        group, chunk = place_of(i)
        value = acc[group]
        for q in range(4):
            value = value + jnp.dot(
                hid[q, i],
                down[pl.ds(pl.multiple_of(q * quarter + chunk * CHUNK, CHUNK), CHUNK), :],
                preferred_element_type=f32,
            )
        acc[group] = value

    def wait_mate(i):
        two = hid.at[pl.ds(2 * (1 - core), 2), i]
        tp_copy(two, two, mate, 3, hm_recv.at[lax.rem(i, RING)]).wait_recv()

    weights[1].wait()
    weights[2].wait()
    multiply(0)
    pair_copy(0).start()

    hfloat = hkeep[...].astype(f32)
    contract = (((1,), (1,)), ((), ()))
    side[0:EXPERTS, 0:tok] = lax.dot_general(
        router[...].astype(f32),
        hfloat * gain[...].astype(f32).reshape(1, width),
        contract,
        precision=lax.Precision.HIGHEST,
        preferred_element_type=f32,
    )
    side[EXPERTS:8, 0:tok] = lax.dot_general(
        jnp.ones((8, width), f32),
        hfloat * hfloat,
        contract,
        precision=lax.Precision.HIGHEST,
        preferred_element_type=f32,
    )[EXPERTS:8]

    def side_copy(k):
        return pltpu.make_async_remote_copy(
            src_ref=side,
            dst_ref=side_all.at[k - 1],
            send_sem=side_send.at[k - 1],
            recv_sem=side_recv.at[k - 1],
            device_id={"tp": lax.rem(lane + k, n_tp)},
            device_id_type=MESH,
        )

    for k in range(1, n_tp):
        side_copy(k).start()

    def inv_copy(k):
        return ep_copy(inv_out.at[slot_of[k]], inv_all, slot_of[k], inv_send.at[k - 1], inv_recv, peers[k])

    def finish_side():
        total = side[...]
        for k in range(1, n_tp):
            side_copy(k).wait_recv()
            total = total + side_all[k - 1]
        total = total[:, 0:tok]
        inverse = lax.rsqrt(total[EXPERTS : EXPERTS + 1] / depth + 1e-05)
        logits = total * inverse
        first = jnp.sum(named[0] * logits, axis=0, keepdims=True)
        second = jnp.sum(named[1] * logits, axis=0, keepdims=True)
        leading = jax.nn.sigmoid(first - second)
        mix = named[0] * leading + named[1] * (1.0 - leading)
        inverse_cols = jnp.transpose(jnp.broadcast_to(inverse, (128, tok)))
        spread = jnp.dot(
            disp[0 : 4 * PAD],
            inverse_cols,
            precision=lax.Precision.HIGHEST,
            preferred_element_type=f32,
        )
        for g in range(4):
            inv_out[g] = spread[g * PAD : (g + 1) * PAD]
        inv_all[0] = spread[:PAD]
        for k in range(1, n_ep):
            inv_copy(k).start()
        places = [row_of(named[2], k) for k in range(4)] + [row_of(mix, k) for k in range(4)]
        cols[...] = jnp.transpose(
            jnp.concatenate(places + [jnp.zeros((120, tok), f32)], axis=0)
        )

    shifted = jnp.where(
        lax.broadcasted_iota(jnp.int32, (PAD, PAD), 0)
        == lax.broadcasted_iota(jnp.int32, (PAD, PAD), 1) + SHIFT,
        1.0,
        0.0,
    ).astype(bf16)

    def take_rows(g):
        x_copy(0, g, me).wait_recv()
        x_high[g] = jnp.dot(shifted, x_all[g], preferred_element_type=f32).astype(bf16)

    def ret_copy(g):
        k = peer_of[g]
        return ep_copy(outb.at[g], ret, k, ret_send.at[g - 1], ret_recv, peers[k])

    lane_i = lax.broadcasted_iota(jnp.int32, (tok, PAD), 1).astype(f32)

    def returned(k, value):
        chosen = jnp.where(cols[:, k : k + 1] == lane_i, 1.0, 0.0).astype(bf16)
        return cols[:, 4 + k : 5 + k] * jnp.dot(chosen, value, preferred_element_type=f32)

    def within(i, when, act):
        if when is None:
            return
        if when:
            act()
        else:
            pl.when(jnp.logical_and(i >= 0, i < units))(act)

    def step(s, multiplying, others):
        i_down, i_pass, i_sum, i_far = s - LAG_DOWN, s - LAG_PASS, s - LAG_SUM, s - 1

        for g in range(1, 4):

            @pl.when(s == g * count - HOLD)
            def _():
                take_rows(g)

            @pl.when(s == g * count - HOLD + LAG_SUM)
            def _():
                inv_copy(peer_of[g]).wait_recv()

        @pl.when(s == LAG_SUM)
        def _():
            finish_side()

        def do_far():
            pair_copy(i_far).wait_recv()
            pass_far(i_far)
            far_copy(i_far).start()

        def do_sum():
            far_copy(i_sum).wait_recv()
            activate(i_sum)
            hid_across(i_sum, own_q).start()
            hid_mate(i_sum, own_q, 3).start()

        def do_pass():
            hid_across(i_pass, far_q).wait_recv()
            hid_mate(i_pass, far_q, 4).start()

        def do_down():
            wait_mate(i_down)
            descend(i_down)

        def do_both():
            wait_mate(i_down)
            multiply(s)
            descend(i_down)
            pair_copy(s).start()

        within(i_far, others, do_far)
        within(i_sum, others, do_sum)
        within(i_pass, others, do_pass)
        if multiplying and others:
            do_both()
        else:
            if multiplying:
                multiply(s)
                pair_copy(s).start()
            within(i_down, others, do_down)

        for g in range(1, 4):

            @pl.when(i_down == (g + 1) * count - 1 - HOLD)
            def _():
                outb[g] = acc[g].astype(bf16)
                ret_copy(g).start()

    def early(s, carry):
        step(s, True, False)
        return carry

    def steady(s, carry):
        step(s, True, True)
        return carry

    def late(s, carry):
        step(s, False, False)
        return carry

    lax.fori_loop(1, LAG_DOWN, early, 0)
    weights[3].wait()
    lax.fori_loop(LAG_DOWN, units, steady, 0)
    lax.fori_loop(units, units + LAG_DOWN, late, 0)

    result = hkeep[...].astype(f32) + returned(0, acc[0].astype(bf16))
    for k in (2, 3, 1):
        ep_copy(outb.at[1], ret, k, ret_send.at[0], ret_recv, me).wait_recv()
        result = result + returned(k, ret[k])
    out_ref[...] = result.astype(bf16)

    for copy in ctx_sends + x_sends:
        copy.wait_send()
    for n in range(4):
        part_copy(n).wait_send()
        if n:
            land_copy(n).wait_send()

    @pl.when(jnp.logical_not(at_home))
    def _():
        land_copy(0).wait_send()

    for k in range(1, 4):
        side_copy(k).wait_send()
        inv_copy(k).wait_send()
        ret_copy(k).wait_send()
    tp_copy(pair_out, pair_in, mate, 0, pair_recv.at[0]).wait_send()
    tp_copy(far_out, far_in, across, 1, far_recv.at[0]).wait_send()
    for q, target, number in ((own_q, across, 2), (own_q, mate, 3), (far_q, mate, 4)):
        tp_copy(hid.at[q], hid.at[q], target, number, hx_recv.at[0]).wait_send()


def fused_device(context, stream, out_proj, norm_gain, router, expert_ids, w_gate, w_up, w_down):
    n_ep, n_tp = lax.axis_size("ep"), lax.axis_size("tp")
    tok, width = stream.shape
    heads = context.shape[1]
    units = n_ep * (w_gate.shape[1] // n_tp // CHUNK)
    bf16, f32 = jnp.bfloat16, jnp.float32
    hbm = pl.BlockSpec(memory_space=pl.ANY)
    vmem = pl.BlockSpec(memory_space=pltpu.VMEM)
    arrays = [
        ((n_ep, tok, heads), bf16),
        (stream.shape, bf16),
        (norm_gain.shape, bf16),
        (router.shape[::-1], bf16),
        (expert_ids.shape[::-1], jnp.int32),
        (out_proj.shape, bf16),
        (w_gate.shape, bf16),
        (w_up.shape, bf16),
        (w_down.shape, bf16),
        ((5 * PAD, tok), f32),
        ((n_ep, 2, tok, width // 2), bf16),
        ((n_ep, tok, width // 2), bf16),
        ((n_ep, tok, width // 2), bf16),
        ((n_tp, tok, width // 2), bf16),
        ((tok, width), bf16),
        ((n_ep, PAD, width), bf16),
        ((n_ep, PAD, width), bf16),
        ((n_ep, PAD, width), bf16),
        ((8, 128), f32),
        ((n_tp - 1, 8, 128), f32),
        ((3, 8, tok), f32),
        ((n_ep, PAD, 128), f32),
        ((n_ep, PAD, 128), f32),
        ((tok, 128), f32),
        ((units, 2, PACK, CHUNK), bf16),
        ((units, 2, PACK, CHUNK), bf16),
        ((2, PACK, CHUNK), f32),
        ((units, PACK, CHUNK), f32),
        ((units, PACK, CHUNK), bf16),
        ((units, PACK, CHUNK), bf16),
        ((n_tp, units, PAD, CHUNK), bf16),
        ((n_ep, PAD, width), f32),
        ((n_ep, PAD, width), bf16),
        ((n_ep, PAD, width), bf16),
    ]
    scratch = [pltpu.VMEM(shape, kind) for shape, kind in arrays]
    for size in (5, 4, 3, 4, 4, 4, 4, 4, 3, 3, 3, 4, 3, 4, 3, 4, 5, RING, RING, RING, RING):
        scratch.append(pltpu.SemaphoreType.DMA((size,)))
    return pl.pallas_call(
        functools.partial(fused_kernel, n_ep, n_tp),
        out_shape=jax.ShapeDtypeStruct((tok, width), bf16),
        in_specs=[hbm] * 9,
        out_specs=vmem,
        scratch_shapes=scratch,
        compiler_params=pltpu.CompilerParams(
            collective_id=0, has_side_effects=True, vmem_limit_bytes=VMEM_BYTES
        ),
        name="fused_layer",
    )(context, stream, norm_gain, router.T, expert_ids.T, out_proj, w_gate, w_up, w_down)


def solution(mesh):
    sizes = dict(mesh.shape)
    fused = sizes["tp"] == 4 and sizes["ep"] == EXPERTS
    return jax.shard_map(
        fused_device if fused else plain_device,
        mesh=mesh,
        in_specs=(
            P(("groups", "ep"), "tp"),
            P(("groups", "ep"), "tp"),
            P("tp", "ep"),
            P("tp"),
            P("tp", None),
            P(("groups", "ep"), None),
            P("tp", "ep"),
            P("tp", "ep"),
            P("ep", "tp"),
        ),
        out_specs=P(("groups", "ep"), "tp"),
        check_vma=False,
    )
```

time: 89.4 us -> 111 us (1.24)
  Pallas kernels: 87.6 us -> 109 us
    pallas_call x1, Pallas kernels: 87.6 us -> 109 us  [fused_device(): pl.pallas_call(functools.partial(fused_kernel, n_ep, n_tp), out_shape=jax...]
where the time goes in v1:
time: 111 us
  Pallas kernels  109 us (98%)
  local copies, waits for them, and re-layouts  1.57 us (1%)
    pallas_call x1, Pallas kernels, fused_device(): pl.pallas_call(functools.partial(fused_kernel, n_ep, n_tp), out_shape=jax...  109 us

profile of v1, /device:TPU:0, one launch (start us, length us, event | category | flops | bytes accessed | tf_op | source)
XLA Modules:
  0.0 111.0 jit_solution(13822346623315920897)
XLA Ops:
  0.0 109.5 %fused_layer.1 = bf16[64,1024]{1,0:T(8,128)(2,1)} custom-call(bf16[64,1024]{1,0:T(8,128)(2,1)} %ctx_hbm.1, bf16[64,1024]{1,0:T(8,128)(2,1)} %stream_hbm.1, bf16[1024]{0:T(1024)(128)(2,1)} %gain_hbm.1, bf16[4,1024]{1,0:T(4,128)(2,1)} %bitcast.2, s32[2,64]{1,0:T(2,128)} %bitcast.3, bf16[1024,1024]{1,0:T(8,128)(2,1)} %proj_hbm.1, bf16[1024,7168]{1,0:T(8,128)(2,1)} %gate_hbm.1, ...), custom_call_target="tpu_custom_call" | custom-call | tf_op jit(solution)/shard_map/fused_layer/pallas_call | solution.py:686
  109.5 1.6 %copy.11 = bf16[64,1024]{1,0:T(8,128)(2,1)} copy(bf16[64,1024]{1,0:T(8,128)(2,1)} %fused_layer.1) | data formatting | bytes 262144

commit v2 on v1

--- a/solution.py
+++ b/solution.py
@@ -95,7 +95,8 @@
 PACK = 2 * CAP
 BASE = PACK - PAD
 HOLD = 2
-LAG_SUM, LAG_PASS, LAG_DOWN = 4, 7, 9
+LAG_SUM, LAG_PASS, LAG_DOWN = 4, 8, 10
+SEND_AT = 1
 RING = 14
 PIECES = 4
 VMEM_BYTES = 67043328
@@ -214,11 +215,16 @@
         smalls.append(copy)
     weights = []
     for number, (src, dst) in enumerate(((proj_hbm, proj), (gate_hbm, gate), (up_hbm, up), (down_hbm, down))):
+        weights.append((src, dst, pltpu.make_async_copy(src, dst, w_sem.at[number])))
+
+    def load(number):
+        src, dst, _ = weights[number]
         step_rows = src.shape[0] // PIECES
         for p in range(PIECES):
             rows = pl.ds(p * step_rows, step_rows)
             pltpu.make_async_copy(src.at[rows], dst.at[rows], w_sem.at[number]).start()
-        weights.append(pltpu.make_async_copy(src, dst, w_sem.at[number]))
+
+    load(0)
 
     smalls[1].wait()
     kinds = lax.broadcasted_iota(jnp.int32, (8, tok), 0)
@@ -242,7 +248,10 @@
     side[...] = jnp.zeros_like(side)
     acc[...] = jnp.zeros_like(acc)
 
-    smalls[0].wait()
+    for n in (0, 2, 3, 4):
+        smalls[n].wait()
+    for n in (1, 2, 3):
+        load(n)
     pl.semaphore_wait(barrier, n_ep * n_tp - 1)
 
     def ep_copy(src, dst, slot, send, recv, target):
@@ -261,7 +270,7 @@
     ctx_sends = (ctx_copy(0, far_k, far_peer), ctx_copy(1, next_k, next_peer), ctx_copy(2, 1, peers[1]))
     for copy in ctx_sends:
         copy.start()
-    weights[0].wait()
+    weights[0][2].wait()
 
     order = (0, 1 + middle, 2 + middle, 3 - 2 * middle)
     owners = (
@@ -321,9 +330,6 @@
             finish_part(n - 1)
     finish_part(3)
 
-    smalls[2].wait()
-    smalls[3].wait()
-    smalls[4].wait()
     for t in range(n_tp):
 
         @pl.when(jnp.logical_not(jnp.logical_and(at_home, lane == t)))
@@ -360,8 +366,6 @@
         )
 
     x_sends = (x_copy(0, far_k - 1, far_peer), x_copy(1, next_k - 1, next_peer), x_copy(2, 3, peers[1]))
-    for copy in x_sends:
-        copy.start()
 
     own_q = 2 * core + side_x
     far_q = 2 * core + (1 - side_x)
@@ -436,8 +440,8 @@
         two = hid.at[pl.ds(2 * (1 - core), 2), i]
         tp_copy(two, two, mate, 3, hm_recv.at[lax.rem(i, RING)]).wait_recv()
 
-    weights[1].wait()
-    weights[2].wait()
+    weights[1][2].wait()
+    weights[2][2].wait()
     multiply(0)
     pair_copy(0).start()
 
@@ -532,6 +536,10 @@
         else:
             pl.when(jnp.logical_and(i >= 0, i < units))(act)
 
+    def send_rows():
+        for copy in x_sends:
+            copy.start()
+
     def step(s, multiplying, others):
         i_down, i_pass, i_sum, i_far = s - LAG_DOWN, s - LAG_PASS, s - LAG_SUM, s - 1
 
@@ -544,6 +552,10 @@
             @pl.when(s == g * count - HOLD + LAG_SUM)
             def _():
                 inv_copy(peer_of[g]).wait_recv()
+
+        @pl.when(s == SEND_AT)
+        def _():
+            send_rows()
 
         @pl.when(s == LAG_SUM)
         def _():
@@ -574,15 +586,15 @@
             descend(i_down)
             pair_copy(s).start()
 
+        if multiplying and others:
+            do_both()
+        elif multiplying:
+            multiply(s)
+            pair_copy(s).start()
         within(i_far, others, do_far)
         within(i_sum, others, do_sum)
         within(i_pass, others, do_pass)
-        if multiplying and others:
-            do_both()
-        else:
-            if multiplying:
-                multiply(s)
-                pair_copy(s).start()
+        if not (multiplying and others):
             within(i_down, others, do_down)
 
         for g in range(1, 4):
@@ -605,7 +617,7 @@
         return carry
 
     lax.fori_loop(1, LAG_DOWN, early, 0)
-    weights[3].wait()
+    weights[3][2].wait()
     lax.fori_loop(LAG_DOWN, units, steady, 0)
     lax.fori_loop(units, units + LAG_DOWN, late, 0)
 

time: 111 us -> 81.1 us (0.73)
  Pallas kernels: 109 us -> 79.3 us
    pallas_call x1, Pallas kernels: 109 us -> 79.3 us  [fused_device(): pl.pallas_call(functools.partial(fused_kernel, n_ep, n_tp), out_shape=jax...]
where the time goes in v2:
time: 81.1 us; the launch traced here: 80.9 us
  Pallas kernels  79.3 us (98%)
  local copies, waits for them, and re-layouts  1.57 us (2%)
    pallas_call x1, Pallas kernels, fused_device(): pl.pallas_call(functools.partial(fused_kernel, n_ep, n_tp), out_shape=jax...  79.3 us

profile of v2, /device:TPU:0, one launch (start us, length us, event | category | flops | bytes accessed | tf_op | source)
XLA Modules:
  0.0 80.9 jit_solution(18306225729915209306)
XLA Ops:
  0.0 79.3 %fused_layer.1 = bf16[64,1024]{1,0:T(8,128)(2,1)} custom-call(bf16[64,1024]{1,0:T(8,128)(2,1)} %ctx_hbm.1, bf16[64,1024]{1,0:T(8,128)(2,1)} %stream_hbm.1, bf16[1024]{0:T(1024)(128)(2,1)} %gain_hbm.1, bf16[4,1024]{1,0:T(4,128)(2,1)} %bitcast.2, s32[2,64]{1,0:T(2,128)} %bitcast.3, bf16[1024,1024]{1,0:T(8,128)(2,1)} %proj_hbm.1, bf16[1024,7168]{1,0:T(8,128)(2,1)} %gate_hbm.1, ...), custom_call_target="tpu_custom_call" | custom-call | tf_op jit(solution)/shard_map/fused_layer/pallas_call | solution.py:698
  79.3 1.6 %copy.11 = bf16[64,1024]{1,0:T(8,128)(2,1)} copy(bf16[64,1024]{1,0:T(8,128)(2,1)} %fused_layer.1) | data formatting | bytes 262144
